TPU v7x, 128 devices: a whole 4x4x4 slice. The times are simulated.
128 devices in a mesh: plane: 8 (over z_hi, x), tile: 16 (over z_lo, y, core).
Axes of the slice: x: 4, y: 4, z: 4 (z_hi: 2, z_lo: 2; z = z_hi * 2 + z_lo), core: 2. Of those that a mesh axis runs over, the one named last changes fastest.
Arguments:
- visibility: float32 [2, 262144], P(None, ('plane', 'tile')), may hold values from -6 to 6
- target: int32 [262144, 1], P(('plane', 'tile')), may hold values from 0 to 127; in each aligned block of 2048 rows (0 to 2047, 2048 to 4095, ...) at most 32 rows name the same one
- offset: int32 [262144], P(('plane', 'tile')), may hold values from 0 to 1048575
- taps: float32 [8], replicated, may hold values from 0.1 to 1
- w_plane: float32 [8], P('plane'), may hold values from -300 to 300
Outputs:
- dirty_image: float32 [4096, 4096], P('plane', 'tile')
Inputs may be any that keep to these rules, and one draw needn't show every extreme that they name: `target`: among the rows of one device no value occurs more than 32 times, and some value occurs exactly 32 times.
All inputs are finite; a program needn't handle non-finite values.
Results may differ from a plain program's by a relative error of at most 0.0042.
Values sent between devices are 32-bit elements; how exact they have to be, the bound alone decides.
A program may use at most 128 MiB of HBM per device.

v0:
```python
import math
import jax
import jax.numpy as jnp
from jax import lax
from jax.sharding import Mesh
from jax.sharding import PartitionSpec as P

G = 4096
TILE = ("tile_0", "tile_1", "tile_2")
PLANE = ("plane_0", "plane_1")
PLANE_TILE = ("plane_0", "plane_1", "tile_0", "tile_1", "tile_2")
HIGHEST = lax.Precision.HIGHEST


def split_up(x, dim, length):
    dims = x.shape
    blocks = x.reshape(*dims[:dim], length, dims[dim] // length, *dims[dim + 1 :])
    return jnp.moveaxis(blocks, dim, 0)


def joined_along(blocks, dim):
    blocks = jnp.moveaxis(blocks, 0, dim)
    dims = blocks.shape
    return blocks.reshape(*dims[:dim], dims[dim] * dims[dim + 1], *dims[dim + 2 :])


def moved_by_axis(blocks, axes, sequence):
    dims = [lax.axis_size(a) for a in axes]
    blocks = blocks.reshape(*dims, *blocks.shape[1:])
    for k in sequence:
        blocks = lax.all_to_all(blocks, axes[k], split_axis=k, concat_axis=k, tiled=True)
    return blocks.reshape(-1, *blocks.shape[len(axes) :])


def exchange_by_chip(x, groups, sequence, split_dim, concat_dim):
    length = lax.axis_size(groups[0]) * lax.axis_size(groups[1])
    blocks = split_up(x, split_dim, length)
    return joined_along(moved_by_axis(blocks, groups, sequence), concat_dim)


def shifted(x, axis, by):
    length = lax.axis_size(axis)
    return lax.ppermute(x, axis, [(i, (i + by) % length) for i in range(length)])


def summed_on_arrival(x, axis, dim):
    blocks = split_up(x, dim, lax.axis_size(axis))
    arrived = lax.all_to_all(blocks, axis, split_axis=0, concat_axis=0, tiled=True)
    return arrived.sum(axis=0)


def direction(index, length):
    return ((index + length // 2) % length - length // 2).astype(jnp.float32) * (0.5 / length)


def angle_table(first, second, length):
    product = (
        jnp.arange(first, dtype=jnp.int32)[:, None]
        * jnp.arange(second, dtype=jnp.int32)[None, :]
        % length
    )
    angles = product.astype(jnp.float32) * (2.0 * math.pi / length)
    return (jnp.cos(angles), jnp.sin(angles))


def split_length(length):
    inner_len = math.gcd(length, 128)
    return (length // inner_len, inner_len)


def transform_last(real_part, imag_part):
    length = real_part.shape[-1]
    outer_len, inner_len = split_length(length)
    real_grid = real_part.reshape(-1, outer_len, inner_len)
    imag_grid = imag_part.reshape(-1, outer_len, inner_len)
    cos_one, sin_one = angle_table(outer_len, outer_len, outer_len)
    first_re = jnp.einsum("rab,ak->rkb", real_grid, cos_one, precision=HIGHEST) - jnp.einsum(
        "rab,ak->rkb", imag_grid, sin_one, precision=HIGHEST
    )
    first_im = jnp.einsum("rab,ak->rkb", real_grid, sin_one, precision=HIGHEST) + jnp.einsum(
        "rab,ak->rkb", imag_grid, cos_one, precision=HIGHEST
    )
    cos_tw, sin_tw = angle_table(outer_len, inner_len, length)
    twist_re = first_re * cos_tw - first_im * sin_tw
    twist_im = first_re * sin_tw + first_im * cos_tw
    cos_two, sin_two = angle_table(inner_len, inner_len, inner_len)
    out_re = jnp.einsum("rkb,bq->rqk", twist_re, cos_two, precision=HIGHEST) - jnp.einsum(
        "rkb,bq->rqk", twist_im, sin_two, precision=HIGHEST
    )
    out_im = jnp.einsum("rkb,bq->rqk", twist_re, sin_two, precision=HIGHEST) + jnp.einsum(
        "rkb,bq->rqk", twist_im, cos_two, precision=HIGHEST
    )
    return (out_re.reshape(-1, length), out_im.reshape(-1, length))


def transform_first(real_part, imag_part):
    length = real_part.shape[0]
    outer_len, inner_len = split_length(length)
    real_grid = real_part.reshape(outer_len, inner_len, -1)
    imag_grid = imag_part.reshape(outer_len, inner_len, -1)
    cos_one, sin_one = angle_table(outer_len, outer_len, outer_len)
    first_re = jnp.einsum("abc,ak->kbc", real_grid, cos_one, precision=HIGHEST) - jnp.einsum(
        "abc,ak->kbc", imag_grid, sin_one, precision=HIGHEST
    )
    first_im = jnp.einsum("abc,ak->kbc", real_grid, sin_one, precision=HIGHEST) + jnp.einsum(
        "abc,ak->kbc", imag_grid, cos_one, precision=HIGHEST
    )
    cos_tw, sin_tw = angle_table(outer_len, inner_len, length)
    twist_re = first_re * cos_tw[:, :, None] - first_im * sin_tw[:, :, None]
    twist_im = first_re * sin_tw[:, :, None] + first_im * cos_tw[:, :, None]
    cos_two, sin_two = angle_table(inner_len, inner_len, inner_len)
    out_re = jnp.einsum("kbc,bq->qkc", twist_re, cos_two, precision=HIGHEST) - jnp.einsum(
        "kbc,bq->qkc", twist_im, sin_two, precision=HIGHEST
    )
    out_im = jnp.einsum("kbc,bq->qkc", twist_re, sin_two, precision=HIGHEST) + jnp.einsum(
        "kbc,bq->qkc", twist_im, cos_two, precision=HIGHEST
    )
    return (out_re.reshape(length, -1), out_im.reshape(length, -1))


def grid_block(received, taps, start, block_len, band_rows, totals):
    piece = lax.dynamic_slice_in_dim(received, start, block_len, 1)
    encoded = jnp.maximum(piece[2].astype(jnp.int32) - 1, 0)
    band_row = encoded // G
    column = encoded % G
    kernel_len = taps.shape[0]
    taps_low = taps.astype(jnp.bfloat16)
    weight_re = (taps[None, :] * piece[0][:, None]).astype(jnp.bfloat16)
    weight_im = (taps[None, :] * piece[1][:, None]).astype(jnp.bfloat16)
    rel_row = jnp.arange(band_rows, dtype=jnp.int32)[None, :] - band_row[:, None]
    rel_col = (jnp.arange(G, dtype=jnp.int32)[None, :] - column[:, None]) % G
    row_re = jnp.zeros((block_len, band_rows), jnp.bfloat16)
    row_im = jnp.zeros((block_len, band_rows), jnp.bfloat16)
    col_table = jnp.zeros((block_len, G), jnp.bfloat16)
    for tap_index in range(kernel_len):
        row_re = jnp.where(rel_row == tap_index, weight_re[:, tap_index : tap_index + 1], row_re)
        row_im = jnp.where(rel_row == tap_index, weight_im[:, tap_index : tap_index + 1], row_im)
        col_table = jnp.where(rel_col == tap_index, taps_low[tap_index], col_table)
    row_table = jnp.concatenate([row_re, row_im], axis=1)
    return totals + lax.dot_general(
        row_table, col_table, (((0,), (0,)), ((), ())), preferred_element_type=jnp.float32
    )


def local(visibility, target, offset, taps, w_plane):
    tiles = lax.axis_size(TILE)
    planes = lax.axis_size(PLANE)
    devices = tiles * planes
    vis_dev = visibility.shape[1]
    capacity = 2 * vis_dev // devices
    slot_total = devices * capacity
    band = G // tiles
    columns = G // tiles
    kernel_len = taps.shape[0]
    band_rows = band + kernel_len - 1
    destination = target[:, 0]
    onehot = (destination[:, None] == jnp.arange(devices, dtype=jnp.int32)[None, :]).astype(
        jnp.int32
    )
    rank = jnp.sum(jnp.cumsum(onehot, axis=0) * onehot, axis=1) - 1
    slot = destination * capacity + rank
    payload = jnp.stack([visibility[0], visibility[1], offset.astype(jnp.float32) + 1.0])
    outgoing = jnp.zeros((3, slot_total), jnp.float32).at[:, slot].set(payload)
    received = exchange_by_chip(
        outgoing, (("plane_0", "plane_1", "tile_0", "tile_1"), "tile_2"), (1, 0), 1, 1
    )
    block_len = min(512, slot_total)
    empty = jnp.zeros((2 * band_rows, G), jnp.float32)

    def grid_step(index, totals):
        return grid_block(received, taps, index * block_len, block_len, band_rows, totals)

    gridded = lax.fori_loop(0, slot_total // block_len, grid_step, empty)
    gridded = gridded.reshape(2, band_rows, G)
    incoming = shifted(gridded[:, band:], TILE, 1)
    grid_band = gridded[:, :band].at[:, : kernel_len - 1].add(incoming)
    col_re, col_im = transform_last(grid_band[0], grid_band[1])
    stacked = jnp.stack([col_re, col_im]).reshape(2, band, tiles, columns)
    exchanged = lax.all_to_all(stacked, TILE, split_axis=2, concat_axis=1, tiled=True)
    item_count = exchanged.shape[3]
    rows_re, rows_im = transform_first(
        exchanged[0].reshape(G, item_count), exchanged[1].reshape(G, item_count)
    )
    image_parts = jnp.stack([rows_re, rows_im]).reshape(2, G, 1, item_count).reshape(2, G, columns)
    line_pos = jnp.arange(G, dtype=jnp.int32)
    column_pos = lax.axis_index(TILE) * columns + jnp.arange(columns, dtype=jnp.int32)
    cos_row = direction(line_pos, G)
    cos_col = direction(column_pos, G)
    n_minus = (
        jnp.sqrt(1.0 - cos_row[:, None] * cos_row[:, None] - cos_col[None, :] * cos_col[None, :])
        - 1.0
    )
    phase = 2.0 * math.pi * w_plane[0] * n_minus
    screened = jnp.cos(phase) * image_parts[0] - jnp.sin(phase) * image_parts[1]
    summed = summed_on_arrival(screened, PLANE, 0)
    return summed * (1.0 / math.sqrt(vis_dev * devices))


def solution(mesh):
    finer = Mesh(
        mesh.devices.reshape(2, 4, 2, 4, 2), ("plane_0", "plane_1", "tile_0", "tile_1", "tile_2")
    )
    return jax.shard_map(
        local,
        mesh=finer,
        in_specs=(P(None, PLANE_TILE), P(PLANE_TILE, None), P(PLANE_TILE), P(), P(PLANE)),
        out_specs=P(PLANE, TILE),
        check_vma=False,
    )
```

profile of v0, /device:TPU:8, one launch (start us, length us, event | category | flops | bytes accessed | tf_op | source)
XLA Modules:
  0.0 555.1 jit_solution(2011988327328630223)
XLA Ops:
  2.8 6.1 %scatter_custom_fusion = f32[3,4096]{0,1:T(8,128)S(1)} fusion(s32[2048]{0:T(1024)S(1)} %bitcast.168, f32[2048,3]{1,0:T(8,128)S(1)} %copy.69, f32[]{:T(128)} %constant.337.clone.1), kind=kCustom, calls=%fused_computation.153 | custom fusion | bytes 49156 | tf_op jit(solution)/shard_map/scatter | solution.py:163
  16.3 11.7 %all-to-all-start.1 = ((f32[64,1,192]{2,1,0:T(1,128)}), f32[64,1,192]{2,1,0:T(1,128)S(1)}, u32[]{:S(2)}, u32[]{:S(2)}) async-start(f32[64,1,192]{2,1,0:T(1,128)} %reshape.301), calls=%async_computation.1 | async-start | bytes 131072 | tf_op jit(solution)/shard_map/all_to_all | solution.py:31
  28.0 8.6 %all-to-all-done.1 = f32[64,1,192]{2,1,0:T(1,128)S(1)} async-done(((f32[64,1,192]{2,1,0:T(1,128)}), f32[64,1,192]{2,1,0:T(1,128)S(1)}, u32[]{:S(2)}, u32[]{:S(2)}) %all-to-all-start.1) | async-done | bytes 49184 | tf_op jit(solution)/shard_map/all_to_all | solution.py:31
  37.8 175.1 %while.18 = (s32[]{:T(128)}, f32[526,4096]{1,0:T(8,128)}, f32[3,4096]{1,0:T(4,128)S(1)}, f32[8]{0:T(128)S(1)}, bf16[8]{0:T(256)(128)(2,1)S(1)}, /*index=5*/s32[]...) while((s32[]{:T(128)}, f32[526,4096]{1,0:T(8,128)}, f32[3,4096]{1,0:T(4,128)S(1)}, ...), condition=%wide.region_5.6_spmd.clone, body=%wide.region_4.5_spmd.clone.sunk | while | flops 2273700864 | bytes 18414876 | solution.py:173
  40.5 17.3 %select_add_fusion.2 = f32[526,4096]{1,0:T(8,128)} fusion(f32[526,4096]{1,0:T(8,128)} %get-tuple-element.356, pred[]{:T(512)S(6)} %compare.38, s32[512]{0:T(512)S(1)} %get-tuple-element.312, bf16[]{:T(256)} %bitcast.130, bf16[]{:T(256)} %bitcast.131, bf16[]{:T(256)} %bitcast.132, bf16[]{:T(256)} %bitcast.133, bf16[]{:T(256)} %bitcast.134, ...), kind=kOutput, calls=%fused_computation.4.clone.1 | convolution fusion | flops 2270310400 | bytes 17776656 | tf_op jit(solution)/shard_map/while/body/eval_jaxpr/dot_general | solution.py:140
  60.5 19.5 %select_add_fusion.2 = f32[526,4096]{1,0:T(8,128)} fusion(f32[526,4096]{1,0:T(8,128)} %get-tuple-element.356, pred[]{:T(512)S(6)} %compare.38, s32[512]{0:T(512)S(1)} %get-tuple-element.312, bf16[]{:T(256)} %bitcast.130, bf16[]{:T(256)} %bitcast.131, bf16[]{:T(256)} %bitcast.132, bf16[]{:T(256)} %bitcast.133, bf16[]{:T(256)} %bitcast.134, ...), kind=kOutput, calls=%fused_computation.4.clone.1 | convolution fusion | flops 2270310400 | bytes 17776656 | tf_op jit(solution)/shard_map/while/body/eval_jaxpr/dot_general | solution.py:140
  82.7 19.5 %select_add_fusion.2 = f32[526,4096]{1,0:T(8,128)} fusion(f32[526,4096]{1,0:T(8,128)} %get-tuple-element.356, pred[]{:T(512)S(6)} %compare.38, s32[512]{0:T(512)S(1)} %get-tuple-element.312, bf16[]{:T(256)} %bitcast.130, bf16[]{:T(256)} %bitcast.131, bf16[]{:T(256)} %bitcast.132, bf16[]{:T(256)} %bitcast.133, bf16[]{:T(256)} %bitcast.134, ...), kind=kOutput, calls=%fused_computation.4.clone.1 | convolution fusion | flops 2270310400 | bytes 17776656 | tf_op jit(solution)/shard_map/while/body/eval_jaxpr/dot_general | solution.py:140
  104.8 19.5 %select_add_fusion.2 = f32[526,4096]{1,0:T(8,128)} fusion(f32[526,4096]{1,0:T(8,128)} %get-tuple-element.356, pred[]{:T(512)S(6)} %compare.38, s32[512]{0:T(512)S(1)} %get-tuple-element.312, bf16[]{:T(256)} %bitcast.130, bf16[]{:T(256)} %bitcast.131, bf16[]{:T(256)} %bitcast.132, bf16[]{:T(256)} %bitcast.133, bf16[]{:T(256)} %bitcast.134, ...), kind=kOutput, calls=%fused_computation.4.clone.1 | convolution fusion | flops 2270310400 | bytes 17776656 | tf_op jit(solution)/shard_map/while/body/eval_jaxpr/dot_general | solution.py:140
  127.0 19.5 %select_add_fusion.2 = f32[526,4096]{1,0:T(8,128)} fusion(f32[526,4096]{1,0:T(8,128)} %get-tuple-element.356, pred[]{:T(512)S(6)} %compare.38, s32[512]{0:T(512)S(1)} %get-tuple-element.312, bf16[]{:T(256)} %bitcast.130, bf16[]{:T(256)} %bitcast.131, bf16[]{:T(256)} %bitcast.132, bf16[]{:T(256)} %bitcast.133, bf16[]{:T(256)} %bitcast.134, ...), kind=kOutput, calls=%fused_computation.4.clone.1 | convolution fusion | flops 2270310400 | bytes 17776656 | tf_op jit(solution)/shard_map/while/body/eval_jaxpr/dot_general | solution.py:140
  149.1 19.5 %select_add_fusion.2 = f32[526,4096]{1,0:T(8,128)} fusion(f32[526,4096]{1,0:T(8,128)} %get-tuple-element.356, pred[]{:T(512)S(6)} %compare.38, s32[512]{0:T(512)S(1)} %get-tuple-element.312, bf16[]{:T(256)} %bitcast.130, bf16[]{:T(256)} %bitcast.131, bf16[]{:T(256)} %bitcast.132, bf16[]{:T(256)} %bitcast.133, bf16[]{:T(256)} %bitcast.134, ...), kind=kOutput, calls=%fused_computation.4.clone.1 | convolution fusion | flops 2270310400 | bytes 17776656 | tf_op jit(solution)/shard_map/while/body/eval_jaxpr/dot_general | solution.py:140
  171.3 19.5 %select_add_fusion.2 = f32[526,4096]{1,0:T(8,128)} fusion(f32[526,4096]{1,0:T(8,128)} %get-tuple-element.356, pred[]{:T(512)S(6)} %compare.38, s32[512]{0:T(512)S(1)} %get-tuple-element.312, bf16[]{:T(256)} %bitcast.130, bf16[]{:T(256)} %bitcast.131, bf16[]{:T(256)} %bitcast.132, bf16[]{:T(256)} %bitcast.133, bf16[]{:T(256)} %bitcast.134, ...), kind=kOutput, calls=%fused_computation.4.clone.1 | convolution fusion | flops 2270310400 | bytes 17776656 | tf_op jit(solution)/shard_map/while/body/eval_jaxpr/dot_general | solution.py:140
  193.5 19.5 %select_add_fusion.2 = f32[526,4096]{1,0:T(8,128)} fusion(f32[526,4096]{1,0:T(8,128)} %get-tuple-element.356, pred[]{:T(512)S(6)} %compare.38, s32[512]{0:T(512)S(1)} %get-tuple-element.312, bf16[]{:T(256)} %bitcast.130, bf16[]{:T(256)} %bitcast.131, bf16[]{:T(256)} %bitcast.132, bf16[]{:T(256)} %bitcast.133, bf16[]{:T(256)} %bitcast.134, ...), kind=kOutput, calls=%fused_computation.4.clone.1 | convolution fusion | flops 2270310400 | bytes 17776656 | tf_op jit(solution)/shard_map/while/body/eval_jaxpr/dot_general | solution.py:140
  213.0 7.6 %reshape.264 = f32[2,263,4096]{2,1,0:T(8,128)} reshape(f32[526,4096]{1,0:T(8,128)} %get-tuple-element.158) | data formatting | bytes 17235968 | tf_op jit(solution)/shard_map/reshape | solution.py:174
  221.7 7.6 %slice.405 = f32[2,256,4096]{2,1,0:T(8,128)} slice(f32[2,263,4096]{2,1,0:T(8,128)} %reshape.264), slice={[0:2], [0:256], [0:4096]} | slice | bytes 16777216 | tf_op jit(solution)/shard_map/slice | solution.py:176
  250.3 5.1 subtract_bitcast_fusion.1
  255.4 6.2 %fusion.84 = f32[128,256,32]{1,0,2:T(8,128)S(1)} fusion(f32[256,32,128]{2,1,0:T(8,128)S(1)} %get-tuple-element.234), kind=kOutput, calls=%fused_computation.135 | convolution fusion | flops 1610842112 | bytes 8388608 | tf_op jit(solution)/shard_map/rkb,bq->rqk/dot_general | solution.py:87
  261.7 6.2 %fusion.82 = f32[128,256,32]{1,0,2:T(8,128)S(1)} fusion(f32[256,32,128]{2,1,0:T(8,128)S(1)} %get-tuple-element.234), kind=kOutput, calls=%fused_computation.133 | convolution fusion | flops 1610842112 | bytes 8388608 | tf_op jit(solution)/shard_map/rkb,bq->rqk/dot_general | solution.py:90
  267.9 6.8 %subtract_bitcast_fusion = f32[256,128,32]{0,1,2:T(8,128)S(1)} fusion(f32[128,256,32]{1,0,2:T(8,128)S(1)} %fusion.84, f32[256,32,128]{2,1,0:T(8,128)S(1)} %get-tuple-element.233), kind=kOutput, calls=%fused_computation.114 | convolution fusion | flops 1611890688 | bytes 12582912 | tf_op jit(solution)/shard_map/rkb,bq->rqk/dot_general | solution.py:87
  277.1 6.1 %add_bitcast_fusion = f32[256,128,32]{0,1,2:T(8,128)S(1)} fusion(f32[128,256,32]{1,0,2:T(8,128)S(1)} %fusion.82, f32[256,32,128]{2,1,0:T(8,128)S(1)} %get-tuple-element.233), kind=kOutput, calls=%fused_computation.113 | convolution fusion | flops 1611890688 | bytes 12582912 | tf_op jit(solution)/shard_map/rkb,bq->rqk/dot_general | solution.py:90
  290.5 6.6 %all-to-all-start.2 = ((f32[2,256,16,256]{1,3,0,2:T(8,128)}), f32[2,256,16,256]{1,3,0,2:T(8,128)}, u32[]{:S(2)}, u32[]{:S(2)}) async-start(f32[2,256,16,256]{1,3,0,2:T(8,128)} %copy.80), calls=%async_computation.2 | async-start | bytes 16777216 | tf_op jit(solution)/shard_map/all_to_all | solution.py:179
  298.0 112.6 %all-to-all-done.2 = f32[2,256,16,256]{1,3,0,2:T(8,128)} async-done(((f32[2,256,16,256]{1,3,0,2:T(8,128)}), f32[2,256,16,256]{1,3,0,2:T(8,128)}, u32[]{:S(2)}, u32[]{:S(2)}) %all-to-all-start.2) | async-done | bytes 8388640 | tf_op jit(solution)/shard_map/all_to_all | solution.py:179
  410.6 8.7 %copy.81 = f32[2,256,16,256]{3,1,2,0:T(8,128)} copy(f32[2,256,16,256]{1,3,0,2:T(8,128)} %all-to-all-done.2) | data formatting | bytes 16777216 | tf_op jit(solution)/shard_map/all_to_all | solution.py:179
  423.3 5.9 %fusion.76 = f32[32,128,256]{2,0,1:T(8,128)S(1)} fusion(f32[32,128,256]{2,1,0:T(8,128)S(1)} %bitcast.146), kind=kOutput, calls=%fused_computation.127 | convolution fusion | flops 402667520 | bytes 8388608 | tf_op jit(solution)/shard_map/abc,ak->kbc/dot_general | solution.py:102
  429.2 6.6 %fusion.74 = f32[32,128,256]{2,0,1:T(8,128)S(1)} fusion(f32[32,128,256]{2,1,0:T(8,128)S(1)} %bitcast.147), kind=kOutput, calls=%fused_computation.125 | convolution fusion | flops 402667520 | bytes 8388608 | tf_op jit(solution)/shard_map/abc,ak->kbc/dot_general | solution.py:105
  435.8 6.2 %fusion.94 = f32[32,128,256]{2,0,1:T(8,128)S(1)} fusion(f32[32,128,256]{2,0,1:T(8,128)S(1)} %fusion.76, f32[32,128,256]{2,1,0:T(8,128)S(1)} %bitcast.142), kind=kOutput, calls=%fused_computation.141 | convolution fusion | flops 403716096 | bytes 12582912 | tf_op jit(solution)/shard_map/abc,ak->kbc/dot_general | solution.py:102
  441.9 7.9 %multiply_subtract_fusion = (f32[32,128,256]{2,0,1:T(8,128)S(1)}, f32[32,128,256]{2,0,1:T(8,128)S(1)}) fusion(f32[32,128,256]{2,0,1:T(8,128)S(1)} %fusion.94, f32[32,128]{0,1:T(8,128)S(1)} %copy.87, f32[32,128]{0,1:T(8,128)S(1)} %copy.84, f32[32,128,256]{2,0,1:T(8,128)S(1)} %fusion.74, f32[32,128,256]{2,1,0:T(8,128)S(1)} %bitcast.143), kind=kOutput, calls=%fused_computation.112 | convolution fusion | flops 410007552 | bytes 21004288 | tf_op jit(solution)/shard_map/abc,ak->kbc/dot_general | solution.py:105
  449.9 6.0 %fusion.68 = f32[128,32,256]{2,0,1:T(8,128)S(1)} fusion(f32[32,128,256]{2,0,1:T(8,128)S(1)} %get-tuple-element.232), kind=kOutput, calls=%fused_computation.119 | convolution fusion | flops 1610842112 | bytes 8388608 | tf_op jit(solution)/shard_map/kbc,bq->qkc/dot_general | solution.py:112
  455.9 6.5 %fusion.66 = f32[128,32,256]{2,0,1:T(8,128)S(1)} fusion(f32[32,128,256]{2,0,1:T(8,128)S(1)} %get-tuple-element.232), kind=kOutput, calls=%fused_computation.117 | convolution fusion | flops 1610842112 | bytes 8388608 | tf_op jit(solution)/shard_map/kbc,bq->qkc/dot_general | solution.py:115
  462.4 6.0 %fusion.100 = f32[128,32,256]{2,0,1:T(8,128)S(1)} fusion(f32[128,32,256]{2,0,1:T(8,128)S(1)} %fusion.68, f32[32,128,256]{2,0,1:T(8,128)S(1)} %get-tuple-element.231), kind=kOutput, calls=%fused_computation.143 | convolution fusion | flops 1611890688 | bytes 12582912 | tf_op jit(solution)/shard_map/kbc,bq->qkc/dot_general | solution.py:112
  470.8 6.5 %fusion.103 = f32[128,32,256]{2,0,1:T(8,128)S(1)} fusion(f32[128,32,256]{2,0,1:T(8,128)S(1)} %fusion.66, f32[32,128,256]{2,0,1:T(8,128)S(1)} %get-tuple-element.231), kind=kOutput, calls=%fused_computation.144 | convolution fusion | flops 1611890688 | bytes 12582912 | tf_op jit(solution)/shard_map/kbc,bq->qkc/dot_general | solution.py:115
  479.8 16.9 %fusion.65 = f32[8,512,256]{2,1,0:T(8,128)S(1)} fusion(f32[256]{0:T(256)S(1)} %fusion.179, f32[8,512]{1,0:T(8,128)S(1)} %fusion.141, f32[]{:T(128)} %bitcast, f32[8,512,256]{2,1,0:T(8,128)S(1)} %bitcast.150, f32[8,512,256]{2,1,0:T(8,128)S(1)} %bitcast.149), kind=kLoop, calls=%fused_computation.109 | loop fusion | flops 6291456 | bytes 12600324 | tf_op jit(solution)/shard_map/sub | solution.py:194
  496.8 54.5 %all_to_all.31 = f32[8,512,256]{2,1,0:T(8,128)} all-to-all(f32[8,512,256]{2,1,0:T(8,128)S(1)} %fusion.65), channel_id=1, replica_groups=mesh['plane_0'=2,'plane_1'=4,'tile_0'=2,'tile_1'=4,'tile_2'=2] {'plane_0..., dimensions={0} | all-to-all | bytes 8388608 | tf_op jit(solution)/shard_map/all_to_all | solution.py:48
  (125 shorter events, 76.4 us)
Async XLA Ops:
  0.0 1.7 copy-start
  0.0 2.4 copy-start.3
  0.0 2.4 copy-start.1
  1.7 26.3 %copy-start.2 = (f32[8]{0:T(128)S(1)}, f32[8]{0:T(128)}, u32[]{:S(2)}) copy-start(f32[8]{0:T(128)} %param.12) | copy-start | bytes 100
  16.3 20.4 %all-to-all-start.1 = ((f32[64,1,192]{2,1,0:T(1,128)}), f32[64,1,192]{2,1,0:T(1,128)S(1)}, u32[]{:S(2)}, u32[]{:S(2)}) async-start(f32[64,1,192]{2,1,0:T(1,128)} %reshape.301), calls=%async_computation.1 | async-start | bytes 131072 | tf_op jit(solution)/shard_map/all_to_all | solution.py:31
  221.5 7.8 %collective-permute-start = (f32[2,7,4096]{2,1,0:T(8,128)S(1)}, f32[2,7,4096]{2,1,0:T(8,128)S(1)}, u32[]{:S(2)}, u32[]{:S(2)}) collective-permute-start(f32[2,7,4096]{2,1,0:T(8,128)S(1)} %slice.407), channel_id=1, source_target_pairs={{0,1},{1,2},{2,3},{3,4},{4,5},{5,6},{6,7},{7,8},{8,9},{9,10},{10,1... | collective-permute-start | bytes 688136 | tf_op jit(solution)/shard_map/ppermute | solution.py:43
  290.5 120.1 %all-to-all-start.2 = ((f32[2,256,16,256]{1,3,0,2:T(8,128)}), f32[2,256,16,256]{1,3,0,2:T(8,128)}, u32[]{:S(2)}, u32[]{:S(2)}) async-start(f32[2,256,16,256]{1,3,0,2:T(8,128)} %copy.80), calls=%async_computation.2 | async-start | bytes 16777216 | tf_op jit(solution)/shard_map/all_to_all | solution.py:179
where the time goes:
time: 561 us; the launch traced here: 555 us
  matrix products  248 us (44%)
  waiting for transfers between devices  121 us (22%)
  local copies, waits for them, and re-layouts  67.9 us (12%)
  blocking collectives  58.3 us (10%)
  other arithmetic  39.3 us (7%)
  starting transfers between devices  18.4 us (3%)
    dot_general x8, matrix products, grid_block(): lax.dot_general(row_table, col_table, (((0,), (0,)), ((), ())), preferred...  154 us
    all_to_all x1, waiting for transfers between devices, local(): lax.all_to_all(stacked, TILE, split_axis=2, concat_axis=1, tiled=True)  113 us
    all_to_all x1, blocking collectives, summed_on_arrival(): lax.all_to_all(blocks, axis, split_axis=0, concat_axis=0, tiled=True)  54.5 us
    sub x1, other arithmetic, local(): screened = jnp.cos(phase) * image_parts[0] - jnp.sin(phase) * image_parts[1]  16.9 us
    select_n x8, other arithmetic, grid_block(): jnp.where(rel_row == tap_index, weight_re[:, tap_index:tap_index + 1], ro...  12.7 us
    all_to_all x1, starting transfers between devices, moved_by_axis(): lax.all_to_all(blocks, axes[k], split_axis=k, concat_axis=k, tiled=True)  11.7 us
  transfers between devices with their start and end apart: 3, of which 2 were waited for; matrix products, arithmetic and copies ran while one was open for 1% of the time, Pallas kernels for 0%

commit v1 on v0

--- a/solution.py
+++ b/solution.py
@@ -176,7 +176,10 @@
     grid_band = gridded[:, :band].at[:, : kernel_len - 1].add(incoming)
     col_re, col_im = transform_last(grid_band[0], grid_band[1])
     stacked = jnp.stack([col_re, col_im]).reshape(2, band, tiles, columns)
-    exchanged = lax.all_to_all(stacked, TILE, split_axis=2, concat_axis=1, tiled=True)
+    exchanged = jnp.concatenate(
+        lax.all_to_all(jnp.stack(jnp.split(stacked, lax.axis_size(TILE), axis=2)), TILE, 0, 0),
+        axis=1,
+    )
     item_count = exchanged.shape[3]
     rows_re, rows_im = transform_first(
         exchanged[0].reshape(G, item_count), exchanged[1].reshape(G, item_count)

time: 561 us -> 584 us (1.041)
  other arithmetic: 39.3 us -> 52.1 us
  matrix products: 248 us -> 257 us
    unnamed x1 -> x16, other arithmetic: 0.01 us -> 12.9 us
    slice x1 -> x2, local copies, waits for them, and re-layouts: 4.01 us -> 13.3 us  [local(): exchanged[0].reshape(G, item_count)]
    all_to_all x1 -> x0, local copies, waits for them, and re-layouts: 8.69 us -> none  [local(): lax.all_to_all(stacked, TILE, split_axis=2, concat_axis=1, tiled=True)]
where the time goes in v1:
time: 584 us; the launch traced here: 579 us
  matrix products  257 us (44%)
  waiting for transfers between devices  121 us (21%)
  local copies, waits for them, and re-layouts  69.9 us (12%)
  blocking collectives  58.3 us (10%)
  other arithmetic  52.1 us (9%)
  starting transfers between devices  18.7 us (3%)
    dot_general x8, matrix products, grid_block(): lax.dot_general(row_table, col_table, (((0,), (0,)), ((), ())), preferred...  154 us
    all_to_all x1, waiting for transfers between devices, local(): lax.all_to_all(jnp.stack(jnp.split(stacked, lax.axis_size(TILE), axis=2))...  113 us
    all_to_all x1, blocking collectives, summed_on_arrival(): lax.all_to_all(blocks, axis, split_axis=0, concat_axis=0, tiled=True)  54.5 us
    sub x1, other arithmetic, local(): screened = jnp.cos(phase) * image_parts[0] - jnp.sin(phase) * image_parts[1]  16.9 us
    slice x2, local copies, waits for them, and re-layouts, local(): exchanged[0].reshape(G, item_count)  13.3 us
    unnamed x16, other arithmetic  12.9 us
    select_n x8, other arithmetic, grid_block(): jnp.where(rel_row == tap_index, weight_re[:, tap_index:tap_index + 1], ro...  12.7 us
    all_to_all x1, starting transfers between devices, moved_by_axis(): lax.all_to_all(blocks, axes[k], split_axis=k, concat_axis=k, tiled=True)  12 us
  transfers between devices with their start and end apart: 3, of which 2 were waited for; matrix products, arithmetic and copies ran while one was open for 1% of the time, Pallas kernels for 0%

profile of v1, /device:TPU:8, one launch (start us, length us, event | category | flops | bytes accessed | tf_op | source)
XLA Modules:
  0.0 578.8 jit_solution(16028138509123439256)
XLA Ops:
  2.8 6.1 %scatter_custom_fusion = f32[3,4096]{0,1:T(8,128)S(1)} fusion(s32[2048]{0:T(1024)S(1)} %bitcast.259, f32[2048,3]{1,0:T(8,128)S(1)} %copy.99, f32[]{:T(128)} %constant.337.clone.1), kind=kCustom, calls=%fused_computation.182 | custom fusion | bytes 49156 | tf_op jit(solution)/shard_map/scatter | solution.py:163
  16.3 12.0 %all-to-all-start.1 = ((f32[64,1,192]{2,1,0:T(1,128)}), f32[64,1,192]{2,1,0:T(1,128)S(1)}, u32[]{:S(2)}, u32[]{:S(2)}) async-start(f32[64,1,192]{2,1,0:T(1,128)} %reshape.306), calls=%async_computation.1 | async-start | bytes 131072 | tf_op jit(solution)/shard_map/all_to_all | solution.py:31
  28.4 8.6 %all-to-all-done.1 = f32[64,1,192]{2,1,0:T(1,128)S(1)} async-done(((f32[64,1,192]{2,1,0:T(1,128)}), f32[64,1,192]{2,1,0:T(1,128)S(1)}, u32[]{:S(2)}, u32[]{:S(2)}) %all-to-all-start.1) | async-done | bytes 49184 | tf_op jit(solution)/shard_map/all_to_all | solution.py:31
  38.1 175.1 %while.18 = (s32[]{:T(128)}, f32[526,4096]{1,0:T(8,128)}, f32[3,4096]{1,0:T(4,128)S(1)}, f32[8]{0:T(128)S(1)}, bf16[8]{0:T(256)(128)(2,1)S(1)}, /*index=5*/s32[]...) while((s32[]{:T(128)}, f32[526,4096]{1,0:T(8,128)}, f32[3,4096]{1,0:T(4,128)S(1)}, ...), condition=%wide.region_5.6_spmd.clone, body=%wide.region_4.5_spmd.clone.sunk | while | flops 2273700864 | bytes 18414876 | solution.py:173
  40.8 17.3 %select_add_fusion.2 = f32[526,4096]{1,0:T(8,128)} fusion(f32[526,4096]{1,0:T(8,128)} %get-tuple-element.356, pred[]{:T(512)S(6)} %compare.38, s32[512]{0:T(512)S(1)} %get-tuple-element.312, bf16[]{:T(256)} %bitcast.192, bf16[]{:T(256)} %bitcast.193, bf16[]{:T(256)} %bitcast.194, bf16[]{:T(256)} %bitcast.195, bf16[]{:T(256)} %bitcast.196, ...), kind=kOutput, calls=%fused_computation.4.clone.1 | convolution fusion | flops 2270310400 | bytes 17776656 | tf_op jit(solution)/shard_map/while/body/eval_jaxpr/dot_general | solution.py:140
  60.8 19.5 %select_add_fusion.2 = f32[526,4096]{1,0:T(8,128)} fusion(f32[526,4096]{1,0:T(8,128)} %get-tuple-element.356, pred[]{:T(512)S(6)} %compare.38, s32[512]{0:T(512)S(1)} %get-tuple-element.312, bf16[]{:T(256)} %bitcast.192, bf16[]{:T(256)} %bitcast.193, bf16[]{:T(256)} %bitcast.194, bf16[]{:T(256)} %bitcast.195, bf16[]{:T(256)} %bitcast.196, ...), kind=kOutput, calls=%fused_computation.4.clone.1 | convolution fusion | flops 2270310400 | bytes 17776656 | tf_op jit(solution)/shard_map/while/body/eval_jaxpr/dot_general | solution.py:140
  83.0 19.5 %select_add_fusion.2 = f32[526,4096]{1,0:T(8,128)} fusion(f32[526,4096]{1,0:T(8,128)} %get-tuple-element.356, pred[]{:T(512)S(6)} %compare.38, s32[512]{0:T(512)S(1)} %get-tuple-element.312, bf16[]{:T(256)} %bitcast.192, bf16[]{:T(256)} %bitcast.193, bf16[]{:T(256)} %bitcast.194, bf16[]{:T(256)} %bitcast.195, bf16[]{:T(256)} %bitcast.196, ...), kind=kOutput, calls=%fused_computation.4.clone.1 | convolution fusion | flops 2270310400 | bytes 17776656 | tf_op jit(solution)/shard_map/while/body/eval_jaxpr/dot_general | solution.py:140
  105.1 19.5 %select_add_fusion.2 = f32[526,4096]{1,0:T(8,128)} fusion(f32[526,4096]{1,0:T(8,128)} %get-tuple-element.356, pred[]{:T(512)S(6)} %compare.38, s32[512]{0:T(512)S(1)} %get-tuple-element.312, bf16[]{:T(256)} %bitcast.192, bf16[]{:T(256)} %bitcast.193, bf16[]{:T(256)} %bitcast.194, bf16[]{:T(256)} %bitcast.195, bf16[]{:T(256)} %bitcast.196, ...), kind=kOutput, calls=%fused_computation.4.clone.1 | convolution fusion | flops 2270310400 | bytes 17776656 | tf_op jit(solution)/shard_map/while/body/eval_jaxpr/dot_general | solution.py:140
  127.3 19.5 %select_add_fusion.2 = f32[526,4096]{1,0:T(8,128)} fusion(f32[526,4096]{1,0:T(8,128)} %get-tuple-element.356, pred[]{:T(512)S(6)} %compare.38, s32[512]{0:T(512)S(1)} %get-tuple-element.312, bf16[]{:T(256)} %bitcast.192, bf16[]{:T(256)} %bitcast.193, bf16[]{:T(256)} %bitcast.194, bf16[]{:T(256)} %bitcast.195, bf16[]{:T(256)} %bitcast.196, ...), kind=kOutput, calls=%fused_computation.4.clone.1 | convolution fusion | flops 2270310400 | bytes 17776656 | tf_op jit(solution)/shard_map/while/body/eval_jaxpr/dot_general | solution.py:140
  149.5 19.5 %select_add_fusion.2 = f32[526,4096]{1,0:T(8,128)} fusion(f32[526,4096]{1,0:T(8,128)} %get-tuple-element.356, pred[]{:T(512)S(6)} %compare.38, s32[512]{0:T(512)S(1)} %get-tuple-element.312, bf16[]{:T(256)} %bitcast.192, bf16[]{:T(256)} %bitcast.193, bf16[]{:T(256)} %bitcast.194, bf16[]{:T(256)} %bitcast.195, bf16[]{:T(256)} %bitcast.196, ...), kind=kOutput, calls=%fused_computation.4.clone.1 | convolution fusion | flops 2270310400 | bytes 17776656 | tf_op jit(solution)/shard_map/while/body/eval_jaxpr/dot_general | solution.py:140
  171.6 19.5 %select_add_fusion.2 = f32[526,4096]{1,0:T(8,128)} fusion(f32[526,4096]{1,0:T(8,128)} %get-tuple-element.356, pred[]{:T(512)S(6)} %compare.38, s32[512]{0:T(512)S(1)} %get-tuple-element.312, bf16[]{:T(256)} %bitcast.192, bf16[]{:T(256)} %bitcast.193, bf16[]{:T(256)} %bitcast.194, bf16[]{:T(256)} %bitcast.195, bf16[]{:T(256)} %bitcast.196, ...), kind=kOutput, calls=%fused_computation.4.clone.1 | convolution fusion | flops 2270310400 | bytes 17776656 | tf_op jit(solution)/shard_map/while/body/eval_jaxpr/dot_general | solution.py:140
  193.8 19.5 %select_add_fusion.2 = f32[526,4096]{1,0:T(8,128)} fusion(f32[526,4096]{1,0:T(8,128)} %get-tuple-element.356, pred[]{:T(512)S(6)} %compare.38, s32[512]{0:T(512)S(1)} %get-tuple-element.312, bf16[]{:T(256)} %bitcast.192, bf16[]{:T(256)} %bitcast.193, bf16[]{:T(256)} %bitcast.194, bf16[]{:T(256)} %bitcast.195, bf16[]{:T(256)} %bitcast.196, ...), kind=kOutput, calls=%fused_computation.4.clone.1 | convolution fusion | flops 2270310400 | bytes 17776656 | tf_op jit(solution)/shard_map/while/body/eval_jaxpr/dot_general | solution.py:140
  213.3 7.6 %reshape.268 = f32[2,263,4096]{2,1,0:T(8,128)} reshape(f32[526,4096]{1,0:T(8,128)} %get-tuple-element.158) | data formatting | bytes 17235968 | tf_op jit(solution)/shard_map/reshape | solution.py:174
  222.0 7.6 %slice.405 = f32[2,256,4096]{2,1,0:T(8,128)} slice(f32[2,263,4096]{2,1,0:T(8,128)} %reshape.268), slice={[0:2], [0:256], [0:4096]} | slice | bytes 16777216 | tf_op jit(solution)/shard_map/slice | solution.py:176
  255.5 6.4 %fusion.84 = f32[128,256,32]{1,0,2:T(8,128)S(1)} fusion(f32[256,32,128]{2,1,0:T(8,128)S(1)} %get-tuple-element.234), kind=kOutput, calls=%fused_computation.164 | convolution fusion | flops 1610842112 | bytes 8388608 | tf_op jit(solution)/shard_map/rkb,bq->rqk/dot_general | solution.py:87
  262.0 6.2 %fusion.82 = f32[128,256,32]{1,0,2:T(8,128)S(1)} fusion(f32[256,32,128]{2,1,0:T(8,128)S(1)} %get-tuple-element.234), kind=kOutput, calls=%fused_computation.162 | convolution fusion | flops 1610842112 | bytes 8388608 | tf_op jit(solution)/shard_map/rkb,bq->rqk/dot_general | solution.py:90
  268.2 6.5 %subtract_bitcast_fusion = f32[256,128,32]{0,1,2:T(8,128)S(1)} fusion(f32[128,256,32]{1,0,2:T(8,128)S(1)} %fusion.84, f32[256,32,128]{2,1,0:T(8,128)S(1)} %get-tuple-element.233), kind=kOutput, calls=%fused_computation.143 | convolution fusion | flops 1611890688 | bytes 12582912 | tf_op jit(solution)/shard_map/rkb,bq->rqk/dot_general | solution.py:87
  277.1 6.2 %add_bitcast_fusion = f32[256,128,32]{0,1,2:T(8,128)S(1)} fusion(f32[128,256,32]{1,0,2:T(8,128)S(1)} %fusion.82, f32[256,32,128]{2,1,0:T(8,128)S(1)} %get-tuple-element.233), kind=kOutput, calls=%fused_computation.142 | convolution fusion | flops 1611890688 | bytes 12582912 | tf_op jit(solution)/shard_map/rkb,bq->rqk/dot_general | solution.py:90
  299.6 6.6 %all-to-all-start.2 = ((f32[16,2,256,1,256]{2,4,1,3,0:T(8,128)}), f32[16,2,256,1,256]{2,4,1,3,0:T(8,128)}, u32[]{:S(2)}, u32[]{:S(2)}) async-start(f32[16,2,256,1,256]{2,4,1,3,0:T(8,128)} %fusion.127), calls=%async_computation.2 | async-start | bytes 16777216 | tf_op jit(solution)/shard_map/all_to_all | solution.py:180
  307.0 112.6 %all-to-all-done.2 = f32[16,2,256,1,256]{2,4,1,3,0:T(8,128)} async-done(((f32[16,2,256,1,256]{2,4,1,3,0:T(8,128)}), f32[16,2,256,1,256]{2,4,1,3,0:T(8,128)}, u32[]{:S(2)}, u32[]{:S(2)}) %all-to-all-start.2) | async-done | bytes 8388640 | tf_op jit(solution)/shard_map/all_to_all | solution.py:180
  419.6 7.6 %fusion.264 = (f32[1,16,256,1,256]{2,4,0,3,1:T(8,128)}, f32[1,16,256,1,256]{2,4,0,3,1:T(8,128)}) fusion(f32[2,16,256,1,256]{2,4,0,3,1:T(8,128)} %bitcast.41), kind=kLoop, calls=%fused_computation.359 | loop fusion | bytes 16777216 | tf_op jit(solution)/shard_map/slice | solution.py:185
  432.5 10.1 %fusion.76 = f32[32,128,256]{2,0,1:T(8,128)} fusion(f32[32,128,256]{2,1,0:T(8,128)} %bitcast.240), kind=kOutput, calls=%fused_computation.156 | convolution fusion | flops 402667520 | bytes 8388608 | tf_op jit(solution)/shard_map/abc,ak->kbc/dot_general | solution.py:102
  442.7 7.0 %fusion.74 = f32[32,128,256]{2,0,1:T(8,128)} fusion(f32[32,128,256]{2,1,0:T(8,128)S(1)} %bitcast.241), kind=kOutput, calls=%fused_computation.154 | convolution fusion | flops 402667520 | bytes 8388608 | tf_op jit(solution)/shard_map/abc,ak->kbc/dot_general | solution.py:105
  449.6 5.7 copy.125
  455.4 10.0 %fusion.94 = f32[32,128,256]{2,0,1:T(8,128)S(1)} fusion(f32[32,128,256]{2,0,1:T(8,128)} %fusion.76, f32[32,128,256]{2,1,0:T(8,128)} %bitcast.234), kind=kOutput, calls=%fused_computation.170 | convolution fusion | flops 403716096 | bytes 12582912 | tf_op jit(solution)/shard_map/abc,ak->kbc/dot_general | solution.py:102
  465.4 7.8 %multiply_subtract_fusion = (f32[32,128,256]{2,0,1:T(8,128)S(1)}, f32[32,128,256]{2,0,1:T(8,128)S(1)}) fusion(f32[32,128,256]{2,0,1:T(8,128)S(1)} %fusion.94, f32[32,128]{0,1:T(8,128)S(1)} %copy.132, f32[32,128]{0,1:T(8,128)S(1)} %copy.129, f32[32,128,256]{2,0,1:T(8,128)S(1)} %copy-done.2, f32[32,128,256]{2,1,0:T(8,128)S(1)} %bitcast.235), kind=kOutput, calls=%fused_computation.141 | convolution fusion | flops 410007552 | bytes 21004288 | tf_op jit(solution)/shard_map/abc,ak->kbc/dot_general | solution.py:105
  473.3 6.0 %fusion.68 = f32[128,32,256]{2,0,1:T(8,128)S(1)} fusion(f32[32,128,256]{2,0,1:T(8,128)S(1)} %get-tuple-element.232), kind=kOutput, calls=%fused_computation.148 | convolution fusion | flops 1610842112 | bytes 8388608 | tf_op jit(solution)/shard_map/kbc,bq->qkc/dot_general | solution.py:112
  479.3 6.2 %fusion.66 = f32[128,32,256]{2,0,1:T(8,128)S(1)} fusion(f32[32,128,256]{2,0,1:T(8,128)S(1)} %get-tuple-element.232), kind=kOutput, calls=%fused_computation.146 | convolution fusion | flops 1610842112 | bytes 8388608 | tf_op jit(solution)/shard_map/kbc,bq->qkc/dot_general | solution.py:115
  485.5 6.4 %fusion.100 = f32[128,32,256]{2,0,1:T(8,128)S(1)} fusion(f32[128,32,256]{2,0,1:T(8,128)S(1)} %fusion.68, f32[32,128,256]{2,0,1:T(8,128)S(1)} %get-tuple-element.231), kind=kOutput, calls=%fused_computation.172 | convolution fusion | flops 1611890688 | bytes 12582912 | tf_op jit(solution)/shard_map/kbc,bq->qkc/dot_general | solution.py:112
  494.4 6.7 %fusion.103 = f32[128,32,256]{2,0,1:T(8,128)S(1)} fusion(f32[128,32,256]{2,0,1:T(8,128)S(1)} %fusion.66, f32[32,128,256]{2,0,1:T(8,128)S(1)} %get-tuple-element.231), kind=kOutput, calls=%fused_computation.173 | convolution fusion | flops 1611890688 | bytes 12582912 | tf_op jit(solution)/shard_map/kbc,bq->qkc/dot_general | solution.py:115
  503.5 16.9 %fusion.65 = f32[8,512,256]{2,1,0:T(8,128)S(1)} fusion(f32[256]{0:T(256)S(1)} %fusion.196, f32[8,512]{1,0:T(8,128)S(1)} %fusion.158, f32[]{:T(128)} %bitcast, f32[8,512,256]{2,1,0:T(8,128)S(1)} %bitcast.243, f32[8,512,256]{2,1,0:T(8,128)S(1)} %bitcast.242), kind=kLoop, calls=%fused_computation.138 | loop fusion | flops 6291456 | bytes 12600324 | tf_op jit(solution)/shard_map/sub | solution.py:197
  520.5 54.5 %all_to_all.21 = f32[8,512,256]{2,1,0:T(8,128)} all-to-all(f32[8,512,256]{2,1,0:T(8,128)S(1)} %fusion.65), channel_id=1, replica_groups=mesh['plane_0'=2,'plane_1'=4,'tile_0'=2,'tile_1'=4,'tile_2'=2] {'plane_0..., dimensions={0} | all-to-all | bytes 8388608 | tf_op jit(solution)/shard_map/all_to_all | solution.py:48
  (146 shorter events, 91.6 us)
Async XLA Ops:
  0.0 1.7 copy-start.3
  0.0 2.4 copy-start.6
  0.0 2.4 copy-start.4
  1.7 26.6 %copy-start.5 = (f32[8]{0:T(128)S(1)}, f32[8]{0:T(128)}, u32[]{:S(2)}) copy-start(f32[8]{0:T(128)} %param.12) | copy-start | bytes 100
  16.3 20.7 %all-to-all-start.1 = ((f32[64,1,192]{2,1,0:T(1,128)}), f32[64,1,192]{2,1,0:T(1,128)S(1)}, u32[]{:S(2)}, u32[]{:S(2)}) async-start(f32[64,1,192]{2,1,0:T(1,128)} %reshape.306), calls=%async_computation.1 | async-start | bytes 131072 | tf_op jit(solution)/shard_map/all_to_all | solution.py:31
  221.9 7.8 %collective-permute-start = (f32[2,7,4096]{2,1,0:T(8,128)S(1)}, f32[2,7,4096]{2,1,0:T(8,128)S(1)}, u32[]{:S(2)}, u32[]{:S(2)}) collective-permute-start(f32[2,7,4096]{2,1,0:T(8,128)S(1)} %slice.407), channel_id=1, source_target_pairs={{0,1},{1,2},{2,3},{3,4},{4,5},{5,6},{6,7},{7,8},{8,9},{9,10},{10,1... | collective-permute-start | bytes 688136 | tf_op jit(solution)/shard_map/ppermute | solution.py:43
  299.6 120.1 %all-to-all-start.2 = ((f32[16,2,256,1,256]{2,4,1,3,0:T(8,128)}), f32[16,2,256,1,256]{2,4,1,3,0:T(8,128)}, u32[]{:S(2)}, u32[]{:S(2)}) async-start(f32[16,2,256,1,256]{2,4,1,3,0:T(8,128)} %fusion.127), calls=%async_computation.2 | async-start | bytes 16777216 | tf_op jit(solution)/shard_map/all_to_all | solution.py:180
  432.5 10.1 %copy-start.1 = (f32[1,16,256,1,256]{4,2,1,3,0:T(8,128)S(1)}, f32[1,16,256,1,256]{4,2,1,3,0:T(8,128)}, u32[]{:S(2)}) copy-start(f32[1,16,256,1,256]{4,2,1,3,0:T(8,128)} %copy.127) | copy-start | bytes 12582916
  455.4 10.0 %copy-start = (f32[1,16,256,1,256]{4,2,1,3,0:T(8,128)S(1)}, f32[1,16,256,1,256]{4,2,1,3,0:T(8,128)}, u32[]{:S(2)}) copy-start(f32[1,16,256,1,256]{4,2,1,3,0:T(8,128)} %copy.125) | copy-start | bytes 12582916
  455.4 10.0 %copy-start.2 = (f32[32,128,256]{2,0,1:T(8,128)S(1)}, f32[32,128,256]{2,0,1:T(8,128)}, u32[]{:S(2)}) copy-start(f32[32,128,256]{2,0,1:T(8,128)} %fusion.74) | copy-start | bytes 12582916
